TPU v7x, 32 devices: a whole 2x2x4 slice. The times are simulated.
32 devices in a mesh: tm: 4 (over x, core), space: 8 (over z, y).
Axes of the slice: x: 2, y: 2, z: 4, core: 2. Of those that a mesh axis runs over, the one named last changes fastest.
Arguments:
- obs_perturb: bfloat16 [4, 32, 1024, 256], P('tm', 'space'), may hold values from -1.796875 to 1.796875
- innovation: float32 [4, 32, 1024], P('tm', 'space'), may hold values from -12 to 12
- error_weight: float32 [4, 32, 1024], P('tm', 'space'), may hold values from 0.5 to 2
- obs_column: int32 [4, 32, 1024], P('tm', 'space'), may hold values from 0 to 31
- obs_count: int32 [4, 32], P('tm', 'space'), may hold values from 64 to 1024, as said below
- radius: int32 [32], P('space'), may hold values from 56 to 80
- states: bfloat16 [8, 1024, 16, 256], P('tm', 'space'), may hold values from -6 to 6
Outputs:
- analysis: bfloat16 [8, 1024, 16, 256], P('tm', 'space')
Inputs may be any that keep to these rules, and one draw needn't show every extreme that they name: `obs_count`: at most 1024; some slot and region holds exactly 1024 in every draw.
All inputs are finite; a program needn't handle non-finite values.
Results may differ from a plain program's by a relative error of at most 0.0065.
Values may be sent and summed in bfloat16 or wider, within the bound.
A program may use at most 64 MiB of HBM per device.

v0:
```python
import functools

import jax
import jax.numpy as jnp
from jax import lax
from jax.experimental import pallas as pl
from jax.experimental.pallas import tpu as pltpu
from jax.sharding import PartitionSpec as P

HC = 32
NS_ITERS = 5
INFLATION = 1.1
HALO = 2
REACH = 2 * HALO + 1
EXTRA = 16
MESH = pl.DeviceIdType.MESH
F32 = jnp.float32
BF16 = jnp.bfloat16


def iota2(shape, dim):
    return lax.broadcasted_iota(jnp.int32, shape, dim)


def pack(matrix, row):
    half = matrix.shape[0] // 2
    a, b, c = matrix[:half, :half], matrix[:half, half:], matrix[half:, half:]
    i, j = iota2((half, half), 0), iota2((half, half), 1)
    top = jnp.concatenate([b, jnp.where(j >= i, a, c)], axis=1)
    diagonal = jnp.sum(jnp.where(i == j, c, 0.0), axis=0, keepdims=True)
    second = jnp.concatenate([diagonal, jnp.zeros_like(diagonal)], axis=1)
    place = iota2((EXTRA, 2 * half), 0)
    extra = jnp.where(place == 0, row, jnp.where(place == 1, second, 0.0))
    return top, extra


def unpack(block):
    half = block.shape[0] - EXTRA
    b, d = block[:half, :half], block[:half, half:]
    row = block[half : half + 1]
    diagonal = block[half + 1 : half + 2, :half]
    i, j = iota2((half, half), 0), iota2((half, half), 1)
    flipped = d.T
    a = jnp.where(j >= i, d, flipped)
    c = jnp.where(i > j, d, jnp.where(i < j, flipped, diagonal))
    matrix = jnp.concatenate(
        [jnp.concatenate([a, b], axis=1), jnp.concatenate([b.T, c], axis=1)], axis=0
    )
    return matrix, row


def split(x):
    high = x.astype(BF16)
    return high, (x - high.astype(F32)).astype(BF16)


def dot3(x, m_high, m_low):
    x_high, x_low = split(x)
    dot = functools.partial(jnp.dot, preferred_element_type=F32)
    return dot(x_high, m_high) + (dot(x_high, m_low) + dot(x_low, m_high))


def transform_parts(gram, vec):
    members = gram.shape[0]
    identity = (iota2(gram.shape, 0) == iota2(gram.shape, 1)).astype(F32)
    system = gram + (members - 1) / INFLATION * identity
    frob = jnp.sqrt(jnp.sum(jnp.sum(system * system, axis=0, keepdims=True), axis=1, keepdims=True))
    product = system * (1.0 / frob)
    inverse = None
    for step in range(NS_ITERS):
        middle = 1.5 * identity - 0.5 * product
        m = split(middle)
        last = step == NS_ITERS - 1
        if inverse is None:
            inverse = middle
            moved = dot3(product, *m)
        elif last:
            inverse = dot3(inverse, *m)
        else:
            both = dot3(jnp.concatenate([product, inverse], axis=0), *m)
            moved, inverse = both[:members], both[members:]
        if not last:
            product = dot3(moved, *m)
    m = split(inverse)
    rows = jnp.broadcast_to(vec, (8, members))
    wbar = dot3(dot3(rows, *m), *m)[0:1] / frob
    spread = inverse * (jnp.sqrt(F32(members - 1.0)) / jnp.sqrt(frob))
    return spread, wbar


def assimilate(
    n_tm, n_space,
    count_hbm, radius_hbm, obs_hbm, innov_hbm, weight_hbm, column_hbm, states_hbm, out_ref,
    count_ref, radius_ref, innov_ref, weight_ref, column_ref, anomaly, means, tmat, obs_v, obs_t, mine, recv, halo_out, halo_in, t_out, t_in,
    load_sem, small_sem, rs_send, rs_recv, halo_send, halo_recv, t_send, b_send, t_recv,
):
    tm, sp = lax.axis_index("tm"), lax.axis_index("space")
    after, before = lax.rem(sp + 1, n_space), lax.rem(sp + n_space - 1, n_space)
    regions, capacity, members = obs_v.shape
    half = members // 2
    targets = regions + 2 * HALO

    loads = [
        pltpu.make_async_copy(obs_hbm.at[0, r], obs_v.at[r], load_sem.at[r]) for r in range(regions)
    ]
    small = [
        pltpu.make_async_copy(src, dst, small_sem.at[n])
        for n, (src, dst) in enumerate(
            [
                (count_hbm, count_ref),
                (radius_hbm, radius_ref),
                (innov_hbm.at[0], innov_ref),
                (weight_hbm.at[0], weight_ref),
                (column_hbm.at[0], column_ref),
                (states_hbm, anomaly),
            ]
        )
    ]
    for load in small[:-1] + loads + small[-1:]:
        load.start()

    barrier = pltpu.get_barrier_semaphore()
    peers = [lax.rem(tm + d, n_tm) for d in range(1, n_tm)]
    greeted = [(p, sp) for p in peers]
    greeted += [(t, s) for s in (before, after) for t in range(n_tm)]
    for t, s in greeted:
        pl.semaphore_signal(barrier, inc=1, device_id={"tm": t, "space": s}, device_id_type=MESH)

    for r in range(regions):
        loads[r].wait()
        obs_t[r] = obs_v[r].T
    for load in small[:-1]:
        load.wait()

    shape = (regions, capacity)
    which = iota2(shape, 0)
    count = jnp.zeros(shape, jnp.int32)
    radius = jnp.zeros(shape, jnp.int32)
    for r in range(regions):
        count = jnp.where(which == r, count_ref[0, r], count)
        radius = jnp.where(which == r, radius_ref[r], radius)
    present = (iota2(shape, 1) < count).astype(F32)
    base = weight_ref[...] * present
    inverse_radius = 1.0 / radius.astype(F32)
    position = column_ref[...].astype(F32) + 0.5 - 0.5 * HC
    weights, pulls = [], []
    for offset in range(-HALO, HALO + 1):
        ratio = jnp.minimum(jnp.abs(position - offset * HC) * inverse_radius, 1.0)
        weight = base * jnp.square(1.0 - ratio * ratio)
        weights.append(weight)
        pulls.append(weight * innov_ref[...])

    first_row = iota2((EXTRA, capacity), 0) == 0

    def gram_of(target):
        total = None
        for r in range(max(0, target - 2 * HALO), min(regions, target + 1)):
            k = target - r
            weight = jnp.broadcast_to(weights[k][r : r + 1], (16, capacity)).astype(BF16)
            pull = jnp.where(first_row, pulls[k][r : r + 1], 0.0).astype(BF16)
            scaled = obs_t[r].reshape(members // 16, 16, capacity) * weight[None]
            left = jnp.concatenate([scaled.reshape(members, capacity), pull], axis=0)
            part = jnp.dot(left, obs_v[r], preferred_element_type=F32)
            total = part if total is None else total + part
        top, extra = pack(total[:members], total[members : members + 1])
        mine[target, :half] = top.astype(BF16)
        mine[target, half:] = extra.astype(BF16)

    def exchange(kind, block_of):
        copies = []
        for d, peer in enumerate(peers):
            copies.append(
                pltpu.make_async_remote_copy(
                    src_ref=mine.at[block_of(peer)],
                    dst_ref=recv.at[kind, tm],
                    send_sem=rs_send.at[kind, d],
                    recv_sem=rs_recv.at[kind, tm],
                    device_id={"tm": peer, "space": sp},
                    device_id_type=MESH,
                )
            )
        return copies

    def collect(kind, block):
        total = mine[block].astype(F32)
        for peer in peers:
            pltpu.make_async_copy(
                recv.at[kind, peer], recv.at[kind, peer], rs_recv.at[kind, peer]
            ).wait()
            total = total + recv[kind, peer].astype(F32)
        return total

    edges = [*range(HALO), *range(targets - HALO, targets)]
    for target in edges:
        gram_of(target)
    pl.semaphore_wait(barrier, len(greeted))
    edge_block = lambda p: lax.rem(p + regions + HALO, targets)
    inner_block = lambda p: p + HALO
    edge_copies = exchange(0, edge_block)
    for copy in edge_copies:
        copy.start()
    inner = list(range(HALO, targets - HALO))
    for target in inner:
        gram_of(target)
    inner_copies = exchange(1, inner_block)
    for copy in inner_copies:
        copy.start()

    small[-1].wait()
    lags, _, rows, _ = anomaly.shape

    def centre_on_mean(n, carry):
        lag, r = n // regions, lax.rem(n, regions)
        x = anomaly[lag, r].astype(F32)
        mean = jnp.sum(x, axis=1, keepdims=True) * (1.0 / members)
        means[lag, r] = mean
        anomaly[lag, r] = (x - mean).astype(BF16)
        return carry

    lax.fori_loop(0, lags * regions, centre_on_mean, 0)

    halo_out[...] = collect(0, edge_block(tm)).astype(BF16)
    halo_copy = pltpu.make_async_remote_copy(
        src_ref=halo_out,
        dst_ref=halo_in,
        send_sem=halo_send,
        recv_sem=halo_recv,
        device_id={"tm": tm, "space": jnp.where(tm < HALO, after, before)},
        device_id_type=MESH,
    )
    halo_copy.start()
    total = collect(1, inner_block(tm))
    halo_copy.wait()
    gram, vec = unpack(total + halo_in[...].astype(F32))
    spread, wbar = transform_parts(gram, vec)
    top, extra = pack(spread, wbar)
    t_out[:half] = top.astype(BF16)
    t_out[half:] = extra.astype(BF16)

    def send_transform(t, s, slot, sem):
        return pltpu.make_async_remote_copy(
            src_ref=t_out,
            dst_ref=t_in.at[slot],
            send_sem=sem,
            recv_sem=t_recv.at[slot],
            device_id={"tm": t, "space": s},
            device_id_type=MESH,
        )

    low = [send_transform(t, before, regions + 1, b_send.at[t]) for t in range(n_tm)]
    high = [send_transform(t, after, 0, b_send.at[t]) for t in range(n_tm)]

    @pl.when(tm == 0)
    def _():
        for copy in low:
            copy.start()

    @pl.when(tm == n_tm - 1)
    def _():
        for copy in high:
            copy.start()

    t_copies = [send_transform(p, sp, tm + 1, t_send.at[d]) for d, p in enumerate(peers)]
    for copy in t_copies:
        copy.start()

    def place(slot, block):
        matrix, row = unpack(block.astype(F32))
        tmat[slot] = (matrix + row).astype(BF16)

    def arrive(slot):
        pltpu.make_async_copy(t_in.at[slot], t_in.at[slot], t_recv.at[slot]).wait()
        place(slot, t_in[slot])

    mid = rows // 2

    def update(r, side):
        part = slice(side * mid, (side + 1) * mid)
        column = (iota2((mid, 1), 0) + side * mid) // (rows // HC)
        blend = jnp.abs((column.astype(F32) + 0.5) / HC - 0.5)
        for lag in range(lags):
            block = anomaly[lag, r, part]

            def apply(slot):
                return lax.dot_general(
                    block, tmat[slot], (((1,), (1,)), ((), ())), preferred_element_type=F32
                )

            centre, beside = apply(r + 1), apply(r + 2 * side)
            mean = means[lag, r, part]
            out_ref[lag, r, part] = (mean + centre + blend * (beside - centre)).astype(BF16)

    place(tm + 1, t_out[...])
    for d in range(1, n_tm):
        arrive(lax.rem(tm + d, n_tm) + 1)
    for r in range(regions):
        for side in range(2):
            if (r, side) not in ((0, 0), (regions - 1, 1)):
                update(r, side)
    arrive(0)
    update(0, 0)
    arrive(regions + 1)
    update(regions - 1, 1)

    for copy in edge_copies + inner_copies + t_copies:
        copy.wait_send()

    @pl.when(tm == 0)
    def _():
        for copy in low:
            copy.wait_send()

    @pl.when(tm == n_tm - 1)
    def _():
        for copy in high:
            copy.wait_send()


def shards(n_tm, n_space, obs, innovation, error_weight, obs_column, obs_count, radius, states):
    _, regions, capacity, members = obs.shape
    assert regions == n_tm and obs.shape[0] == 1
    rows = members // 2 + EXTRA
    lags, columns, levels, _ = states.shape
    shaped = states.reshape(lags, regions, columns // regions * levels, members)
    hbm = pl.BlockSpec(memory_space=pltpu.HBM)
    dma = pltpu.SemaphoreType.DMA
    result = pl.pallas_call(
        functools.partial(assimilate, n_tm, n_space),
        out_shape=pltpu.VMEM(shaped.shape, BF16),
        in_specs=[hbm] * 7,
        out_specs=pl.BlockSpec(memory_space=pltpu.VMEM),
        scratch_shapes=[
            pltpu.SMEM(obs_count.shape, jnp.int32),
            pltpu.SMEM(radius.shape, jnp.int32),
            pltpu.VMEM((regions, capacity), F32),
            pltpu.VMEM((regions, capacity), F32),
            pltpu.VMEM((regions, capacity), jnp.int32),
            pltpu.VMEM(shaped.shape, BF16),
            pltpu.VMEM(shaped.shape[:-1] + (1,), F32),
            pltpu.VMEM((regions + 2, members, members), BF16),
            pltpu.VMEM((regions, capacity, members), BF16),
            pltpu.VMEM((regions, members, capacity), BF16),
            pltpu.VMEM((regions + 2 * HALO, rows, members), BF16),
            pltpu.VMEM((2, n_tm, rows, members), BF16),
            pltpu.VMEM((rows, members), BF16),
            pltpu.VMEM((rows, members), BF16),
            pltpu.VMEM((rows, members), BF16),
            pltpu.VMEM((regions + 2, rows, members), BF16),
            dma((regions,)),
            dma((6,)),
            dma((2, n_tm - 1)),
            dma((2, n_tm)),
            dma,
            dma,
            dma((n_tm - 1,)),
            dma((n_tm,)),
            dma((regions + 2,)),
        ],
        compiler_params=pltpu.CompilerParams(
            collective_id=0, has_side_effects=True, vmem_limit_bytes=67043328 - 2228224
        ),
        name="assimilate",
    )(obs_count, radius, obs, innovation, error_weight, obs_column, shaped)
    return result.reshape(states.shape)


def solution(mesh):
    return jax.shard_map(
        functools.partial(shards, mesh.shape["tm"], mesh.shape["space"]),
        mesh=mesh,
        in_specs=(
            P("tm", "space", None, None),
            P("tm", "space", None),
            P("tm", "space", None),
            P("tm", "space", None),
            P("tm", "space"),
            P("space"),
            P("tm", "space", None, None),
        ),
        out_specs=P("tm", "space", None, None),
        check_vma=False,
    )
```

profile of v0, /device:TPU:1, one launch (start us, length us, event | category | flops | bytes accessed | tf_op | source)
XLA Modules:
  0.0 28.4 jit_solution(9074003531366579849)
XLA Ops:
  0.0 27.1 %assimilate.1 = bf16[2,4,512,256]{3,2,1,0:T(8,128)(2,1)S(1)} custom-call(s32[1,4]{1,0:T(1,128)} %count_hbm.1, s32[4]{0:T(128)} %radius_hbm.1, bf16[1,4,1024,256]{3,2,1,0:T(8,128)(2,1)} %obs_hbm.1, f32[1,4,1024]{2,1,0:T(4,128)} %innov_hbm.1, f32[1,4,1024]{2,1,0:T(4,128)} %weight_hbm.1, s32[1,4,1024]{2,1,0:T(4,128)} %column_hbm.1, bf16[2,4,512,256]{3,2,1,0:T(8,128)(2,1)} %bitcast.3), custom_call_target="tpu_custom_call" | custom-call | tf_op jit(solution)/shard_map/assimilate/pallas_call | solution.py:327
  27.1 1.3 %copy.9 = bf16[2,128,16,256]{3,2,1,0:T(8,128)(2,1)} copy(bf16[2,128,16,256]{3,2,1,0:T(8,128)(2,1)S(1)} %bitcast.2) | data formatting | bytes 4194304
where the time goes:
time: 28.5 us; the launch traced here: 28.4 us
  Pallas kernels  27.1 us (95%)
  local copies, waits for them, and re-layouts  1.32 us (5%)
    pallas_call x1, Pallas kernels, shards(): pl.pallas_call(functools.partial(assimilate, n_tm, n_space), out_shape=pl...  27.1 us
    unnamed x1, local copies, waits for them, and re-layouts  1.32 us

commit v1 on v0

v1 whole, which is shorter than its diff:
```python
import functools

import jax
import jax.numpy as jnp
from jax import lax
from jax.experimental import pallas as pl
from jax.experimental.pallas import tpu as pltpu
from jax.sharding import PartitionSpec as P

HC = 32
NS_ITERS = 5
INFLATION = 1.1
HALO = 2
EXTRA = 16
MESH = pl.DeviceIdType.MESH
F32 = jnp.float32
BF16 = jnp.bfloat16
FWD, BWD, NEAR, FAR = range(4)


def iota2(shape, dim):
    return lax.broadcasted_iota(jnp.int32, shape, dim)


def pack(matrix, row):
    half = matrix.shape[0] // 2
    a, b, c = matrix[:half, :half], matrix[:half, half:], matrix[half:, half:]
    i, j = iota2((half, half), 0), iota2((half, half), 1)
    top = jnp.concatenate([b, jnp.where(j >= i, a, c)], axis=1)
    diagonal = jnp.sum(jnp.where(i == j, c, 0.0), axis=0, keepdims=True)
    second = jnp.concatenate([diagonal, jnp.zeros_like(diagonal)], axis=1)
    place = iota2((EXTRA, 2 * half), 0)
    extra = jnp.where(place == 0, row, jnp.where(place == 1, second, 0.0))
    return top, extra


def unpack(block):
    half = block.shape[0] - EXTRA
    b, d = block[:half, :half], block[:half, half:]
    row = block[half : half + 1]
    diagonal = block[half + 1 : half + 2, :half]
    i, j = iota2((half, half), 0), iota2((half, half), 1)
    flipped = d.T
    a = jnp.where(j >= i, d, flipped)
    c = jnp.where(i > j, d, jnp.where(i < j, flipped, diagonal))
    matrix = jnp.concatenate(
        [jnp.concatenate([a, b], axis=1), jnp.concatenate([b.T, c], axis=1)], axis=0
    )
    return matrix, row


def transform_parts(gram, vec):
    n = gram.shape[0]
    both = lambda x: jnp.sum(jnp.sum(x, axis=0, keepdims=True), axis=1, keepdims=True)
    identity = (iota2(gram.shape, 0) == iota2(gram.shape, 1)).astype(F32)
    system = gram + (n - 1) / INFLATION * identity
    frob = jnp.sqrt(both(system * system))
    inverse_frob = 1.0 / frob
    a = both(system * identity) * (1.0 / n) * inverse_frob
    rest = system * inverse_frob - a * identity
    u = jnp.broadcast_to(vec, (EXTRA, n))
    dot = functools.partial(jnp.dot, preferred_element_type=F32)
    z_one = z_rest = None
    for step in range(NS_ITERS):
        last = step == NS_ITERS - 1
        h = 1.5 - 0.5 * a
        r = rest.astype(BF16)
        left = [] if last else [r]
        if step:
            left.append(z_rest.astype(BF16))
        left.append(u.astype(BF16))
        first = dot(jnp.concatenate(left, axis=0), r)
        turned = h * u - 0.5 * first[-EXTRA:]
        if step:
            z_rest = h * z_rest - (0.5 * z_one) * rest - 0.5 * first[-EXTRA - n : -EXTRA]
            z_one = h * z_one
        else:
            z_rest, z_one = -0.5 * rest, h
        left = [] if last else [first[:n].astype(BF16)]
        left.append(turned.astype(BF16))
        second = dot(jnp.concatenate(left, axis=0), r)
        u = h * turned - 0.5 * second[-EXTRA:]
        if not last:
            rest = (
                (2.25 - 3.0 * a + 0.75 * a * a) * rest
                + (0.75 * a - 1.5) * first[:n]
                + 0.25 * second[:n]
            )
            a = a * h * h
    scale = jnp.sqrt(F32(n - 1.0)) * lax.rsqrt(frob)
    spread = (z_rest + z_one * identity) * scale
    return spread, u[0:1] * inverse_frob


def assimilate(
    n_space,
    count_hbm, radius_hbm, obs_hbm, innov_hbm, weight_hbm, column_hbm, states_hbm, out_ref,
    count_ref, radius_ref, innov_ref, weight_ref, column_ref, anomaly, means, tmat, obs_v, obs_t,
    mine, near_in, edge_out, halo_in, own, cross_out, cross_in, t_out, t_in,
    load_sem, small_sem, near_send, near_recv, edge_send, halo_recv, cross_send, cross_recv,
    t_send, t_recv,
):
    tm, sp = lax.axis_index("tm"), lax.axis_index("space")
    after, before = lax.rem(sp + 1, n_space), lax.rem(sp + n_space - 1, n_space)
    chip, core = tm // 2, lax.rem(tm, 2)
    partner, cross = 2 * chip + 1 - core, 2 * (1 - chip) + core
    regions, capacity, members = obs_v.shape
    half = members // 2
    region_of = lambda t: lax.rem(t + 2, 3) + t // 3
    low_owner, high_owner = 1, 3
    here = lambda t: {"tm": t, "space": sp}

    def remote(src, dst, send, recv, device):
        return pltpu.make_async_remote_copy(
            src_ref=src, dst_ref=dst, send_sem=send, recv_sem=recv, device_id=device, device_id_type=MESH
        )

    def arrived(ref, sem):
        pltpu.make_async_copy(ref, ref, sem).wait()

    loads = [
        pltpu.make_async_copy(obs_hbm.at[0, r], obs_v.at[r], load_sem.at[r]) for r in range(regions)
    ]
    small = [
        pltpu.make_async_copy(src, dst, small_sem.at[n])
        for n, (src, dst) in enumerate(
            [
                (count_hbm, count_ref),
                (radius_hbm, radius_ref),
                (innov_hbm.at[0], innov_ref),
                (weight_hbm.at[0], weight_ref),
                (column_hbm.at[0], column_ref),
                (states_hbm, anomaly),
            ]
        )
    ]
    for load in small[:-1] + loads[::-1] + small[-1:]:
        load.start()

    barrier = pltpu.get_barrier_semaphore()
    peers = [lax.rem(tm + d, 4) for d in range(1, 4)]
    greeted = [(p, sp) for p in peers]
    greeted += [(t, s) for s in (before, after) for t in range(4)]
    for t, s in greeted:
        pl.semaphore_signal(barrier, inc=1, device_id={"tm": t, "space": s}, device_id_type=MESH)

    for load in small[:-1]:
        load.wait()
    shape = (regions, capacity)
    which = iota2(shape, 0)
    count = jnp.zeros(shape, jnp.int32)
    radius = jnp.zeros(shape, jnp.int32)
    for r in range(regions):
        count = jnp.where(which == r, count_ref[0, r], count)
        radius = jnp.where(which == r, radius_ref[r], radius)
    present = (iota2(shape, 1) < count).astype(F32)
    base = weight_ref[...] * present
    inverse_radius = 1.0 / radius.astype(F32)
    position = column_ref[...].astype(F32) + 0.5 - 0.5 * HC
    weights, pulls = [], []
    for offset in range(-HALO, HALO + 1):
        ratio = jnp.minimum(jnp.abs(position - offset * HC) * inverse_radius, 1.0)
        weight = base * jnp.square(1.0 - ratio * ratio)
        weights.append(weight)
        pulls.append(weight * innov_ref[...])

    first_row = iota2((EXTRA, capacity), 0) == 0

    def gram_of(target):
        total = None
        for r in range(max(0, target - 2 * HALO), min(regions, target + 1)):
            k = target - r
            weight = jnp.broadcast_to(weights[k][r : r + 1], (16, capacity)).astype(BF16)
            pull = jnp.where(first_row, pulls[k][r : r + 1], 0.0).astype(BF16)
            scaled = obs_t[r].reshape(members // 16, 16, capacity) * weight[None]
            left = jnp.concatenate([scaled.reshape(members, capacity), pull], axis=0)
            part = jnp.dot(left, obs_v[r], preferred_element_type=F32)
            total = part if total is None else total + part
        top, extra = pack(total[:members], total[members : members + 1])
        mine[target, :half] = top.astype(BF16)
        mine[target, half:] = extra.astype(BF16)

    def near_copy(group, block):
        return remote(
            mine.at[block], near_in.at[group], near_send.at[group], near_recv.at[group], here(partner)
        )

    def chip_sum(group, block):
        arrived(near_in.at[group], near_recv.at[group])
        return mine[block].astype(F32) + near_in[group].astype(F32)

    def edge_copy(group, owner, space):
        edge_out[group] = chip_sum(group, own_block[group]).astype(BF16)
        return remote(
            edge_out.at[group],
            halo_in.at[chip],
            edge_send.at[group],
            halo_recv.at[chip],
            {"tm": owner, "space": space},
        )

    cross_copy = remote(cross_out, cross_in, cross_send, cross_recv, here(cross))

    def settle(group, keep):
        total = chip_sum(group, own_block[group])

        @pl.when(keep)
        def _():
            own[...] = total

        @pl.when(jnp.logical_not(keep))
        def _():
            cross_out[...] = total.astype(BF16)
            cross_copy.start()

    own_block = {FWD: 7 - core, BWD: core, FAR: 4 + core, NEAR: 3 - core}
    partner_block = {FWD: 6 + core, BWD: 1 - core, FAR: 5 - core, NEAR: 2 + core}
    near = {g: near_copy(g, partner_block[g]) for g in (FWD, FAR, NEAR, BWD)}

    with jax.named_scope("p1_fwd"):
        loads[3].wait()
        obs_t[3] = obs_v[3].T
        gram_of(7)
        loads[2].wait()
        obs_t[2] = obs_v[2].T
        gram_of(6)
    with jax.named_scope("p2_barrier"):
        pl.semaphore_wait(barrier, len(greeted))
    near[FWD].start()
    with jax.named_scope("p3_far"):
        for r in (1, 0):
            loads[r].wait()
            obs_t[r] = obs_v[r].T
        gram_of(5)
        gram_of(4)
    near[FAR].start()
    with jax.named_scope("p4_fwdsum"):
        edge_fwd = edge_copy(FWD, 2 - core, after)
    edge_fwd.start()
    with jax.named_scope("p5_near"):
        gram_of(3)
        gram_of(2)
    near[NEAR].start()
    with jax.named_scope("p6_farsum"):
        settle(FAR, chip == core)
    with jax.named_scope("p7_bwd"):
        gram_of(1)
        gram_of(0)
    near[BWD].start()
    with jax.named_scope("p8_nearsum"):
        settle(NEAR, chip != core)

    small[-1].wait()
    lags, _, rows, _ = anomaly.shape

    def centre_on_mean(n, carry):
        lag, r = n // regions, lax.rem(n, regions)
        x = anomaly[lag, r].astype(F32)
        mean = jnp.sum(x, axis=1, keepdims=True) * (1.0 / members)
        means[lag, r] = mean
        anomaly[lag, r] = (x - mean).astype(BF16)
        return carry

    with jax.named_scope("p9_bwdsum"):
        edge_bwd = edge_copy(BWD, 3 * core, before)
    edge_bwd.start()
    with jax.named_scope("q0_centre"):
        lax.fori_loop(0, lags * regions, centre_on_mean, 0)

    with jax.named_scope("q1_cross"):
        arrived(cross_in, cross_recv)
    with jax.named_scope("q2_halo"):
        for x in range(2):
            arrived(halo_in.at[x], halo_recv.at[x])
    with jax.named_scope("q3_ns"):
        total = own[...] + cross_in[...].astype(F32)
        gram, vec = unpack(total + (halo_in[0].astype(F32) + halo_in[1].astype(F32)))
        spread, wbar = transform_parts(gram, vec)
        top, extra = pack(spread, wbar)
        t_out[:half] = top.astype(BF16)
        t_out[half:] = extra.astype(BF16)

    own_slot, cross_slot = region_of(tm) + 1, region_of(cross) + 1
    near_slot, last_slot = region_of(partner) + 1, region_of(2 * (1 - chip) + 1 - core) + 1

    def send_transform(n, slot, device):
        return remote(t_out, t_in.at[slot], t_send.at[n], t_recv.at[slot], device)

    t_cross = send_transform(0, own_slot, here(cross))
    t_near = send_transform(1, own_slot, here(partner))
    order = [1, 0, 3, 2]
    high = [send_transform(2 + n, 0, {"tm": t, "space": after}) for n, t in enumerate(order)]
    low = [send_transform(2 + n, regions + 1, {"tm": t, "space": before}) for n, t in enumerate(order)]
    relay = remote(t_in.at[cross_slot], t_in.at[cross_slot], t_send.at[6], t_recv.at[cross_slot], here(partner))

    t_cross.start()

    @pl.when(tm == low_owner)
    def _():
        for copy in low:
            copy.start()

    @pl.when(tm == high_owner)
    def _():
        for copy in high:
            copy.start()

    t_near.start()

    def place(slot, block):
        matrix, row = unpack(block.astype(F32))
        tmat[slot] = (matrix + row).astype(BF16)

    def wait_slot(slot):
        arrived(t_in.at[slot], t_recv.at[slot])

    mid = rows // 2

    def update(r, side):
        part = slice(side * mid, (side + 1) * mid)
        column = (iota2((mid, 1), 0) + side * mid) // (rows // HC)
        blend = jnp.abs((column.astype(F32) + 0.5) / HC - 0.5)
        for lag in range(lags):
            block = anomaly[lag, r, part]

            def apply(slot):
                return lax.dot_general(
                    block, tmat[slot], (((1,), (1,)), ((), ())), preferred_element_type=F32
                )

            centre, beside = apply(r + 1), apply(r + 2 * side)
            mean = means[lag, r, part]
            out_ref[lag, r, part] = (mean + centre + blend * (beside - centre)).astype(BF16)

    with jax.named_scope("q4_place"):
        place(own_slot, t_out[...])
    with jax.named_scope("q5_near"):
        wait_slot(near_slot)
        place(near_slot, t_in[near_slot])
    with jax.named_scope("q6_cross"):
        wait_slot(cross_slot)
    relay.start()
    with jax.named_scope("q7_last"):
        place(cross_slot, t_in[cross_slot])
        wait_slot(last_slot)
        place(last_slot, t_in[last_slot])
    with jax.named_scope("q8_update"):
        for r in range(regions):
            for side in range(2):
                if (r, side) not in ((0, 0), (regions - 1, 1)):
                    update(r, side)
    with jax.named_scope("q9_wait4"):
        wait_slot(regions + 1)
    with jax.named_scope("r0_upd"):
        place(regions + 1, t_in[regions + 1])
        update(regions - 1, 1)
    with jax.named_scope("r1_wait0"):
        wait_slot(0)
    with jax.named_scope("r2_upd"):
        place(0, t_in[0])
        update(0, 0)

    with jax.named_scope("r3_drain"):
        for copy in (*near.values(), edge_fwd, edge_bwd, cross_copy, t_cross, t_near, relay):
            copy.wait_send()

        @pl.when(tm == low_owner)
        def _():
            for copy in low:
                copy.wait_send()

        @pl.when(tm == high_owner)
        def _():
            for copy in high:
                copy.wait_send()


def shards(n_tm, n_space, obs, innovation, error_weight, obs_column, obs_count, radius, states):
    _, regions, capacity, members = obs.shape
    assert regions == n_tm == 4 and obs.shape[0] == 1
    rows = members // 2 + EXTRA
    lags, columns, levels, _ = states.shape
    shaped = states.reshape(lags, regions, columns // regions * levels, members)
    hbm = pl.BlockSpec(memory_space=pltpu.HBM)
    dma = pltpu.SemaphoreType.DMA
    packed = (rows, members)
    result = pl.pallas_call(
        functools.partial(assimilate, n_space),
        out_shape=pltpu.VMEM(shaped.shape, BF16),
        in_specs=[hbm] * 7,
        out_specs=pl.BlockSpec(memory_space=pltpu.VMEM),
        scratch_shapes=[
            pltpu.SMEM(obs_count.shape, jnp.int32),
            pltpu.SMEM(radius.shape, jnp.int32),
            pltpu.VMEM((regions, capacity), F32),
            pltpu.VMEM((regions, capacity), F32),
            pltpu.VMEM((regions, capacity), jnp.int32),
            pltpu.VMEM(shaped.shape, BF16),
            pltpu.VMEM(shaped.shape[:-1] + (1,), F32),
            pltpu.VMEM((regions + 2, members, members), BF16),
            pltpu.VMEM((regions, capacity, members), BF16),
            pltpu.VMEM((regions, members, capacity), BF16),
            pltpu.VMEM((regions + 2 * HALO, *packed), BF16),
            pltpu.VMEM((4, *packed), BF16),
            pltpu.VMEM((2, *packed), BF16),
            pltpu.VMEM((2, *packed), BF16),
            pltpu.VMEM(packed, F32),
            pltpu.VMEM(packed, BF16),
            pltpu.VMEM(packed, BF16),
            pltpu.VMEM(packed, BF16),
            pltpu.VMEM((regions + 2, *packed), BF16),
            dma((regions,)),
            dma((6,)),
            dma((4,)),
            dma((4,)),
            dma((2,)),
            dma((2,)),
            dma,
            dma,
            dma((7,)),
            dma((regions + 2,)),
        ],
        compiler_params=pltpu.CompilerParams(
            collective_id=0, has_side_effects=True, vmem_limit_bytes=67043328 - 2228224
        ),
        name="assimilate",
    )(obs_count, radius, obs, innovation, error_weight, obs_column, shaped)
    return result.reshape(states.shape)


def solution(mesh):
    return jax.shard_map(
        functools.partial(shards, mesh.shape["tm"], mesh.shape["space"]),
        mesh=mesh,
        in_specs=(
            P("tm", "space", None, None),
            P("tm", "space", None),
            P("tm", "space", None),
            P("tm", "space", None),
            P("tm", "space"),
            P("space"),
            P("tm", "space", None, None),
        ),
        out_specs=P("tm", "space", None, None),
        check_vma=False,
    )
```

time: 28.5 us -> 26 us (0.912)
  the two profiles are of different devices: /device:TPU:1 before, /device:TPU:0 now
where the time goes in v1:
time: 26 us; the launch traced here: 25.8 us
  Pallas kernels  24.5 us (94%)
  local copies, waits for them, and re-layouts  1.32 us (5%)
    pallas_call x1, Pallas kernels, shards(): pl.pallas_call(functools.partial(assimilate, n_space), out_shape=pltpu.VM...  24.5 us
    unnamed x1, local copies, waits for them, and re-layouts  1.32 us

profile of v1, /device:TPU:0, one launch (start us, length us, event | category | flops | bytes accessed | tf_op | source)
XLA Modules:
  0.0 25.8 jit_solution(16868282564360014109)
XLA Ops:
  0.0 24.5 %assimilate.1 = bf16[2,4,512,256]{3,2,1,0:T(8,128)(2,1)S(1)} custom-call(s32[1,4]{1,0:T(1,128)} %count_hbm.1, s32[4]{0:T(128)} %radius_hbm.1, bf16[1,4,1024,256]{3,2,1,0:T(8,128)(2,1)} %obs_hbm.1, f32[1,4,1024]{2,1,0:T(4,128)} %innov_hbm.1, f32[1,4,1024]{2,1,0:T(4,128)} %weight_hbm.1, s32[1,4,1024]{2,1,0:T(4,128)} %column_hbm.1, bf16[2,4,512,256]{3,2,1,0:T(8,128)(2,1)} %bitcast.3), custom_call_target="tpu_custom_call" | custom-call | tf_op jit(solution)/shard_map/assimilate/pallas_call | solution.py:387
  24.5 1.3 %copy.9 = bf16[2,128,16,256]{3,2,1,0:T(8,128)(2,1)} copy(bf16[2,128,16,256]{3,2,1,0:T(8,128)(2,1)S(1)} %bitcast.2) | data formatting | bytes 4194304

commit v2 on v1

--- a/solution.py
+++ b/solution.py
@@ -94,8 +94,8 @@
 
 def assimilate(
     n_space,
-    count_hbm, radius_hbm, obs_hbm, innov_hbm, weight_hbm, column_hbm, states_hbm, out_ref,
-    count_ref, radius_ref, innov_ref, weight_ref, column_ref, anomaly, means, tmat, obs_v, obs_t,
+    count_hbm, radius_hbm, obs_hbm, innov_hbm, weight_hbm, column_hbm, states_hbm, anomaly, means, tmat,
+    count_ref, radius_ref, innov_ref, weight_ref, column_ref, obs_v, obs_t,
     mine, near_in, edge_out, halo_in, own, cross_out, cross_in, t_out, t_in,
     load_sem, small_sem, near_send, near_recv, edge_send, halo_recv, cross_send, cross_recv,
     t_send, t_recv,
@@ -134,7 +134,7 @@
             ]
         )
     ]
-    for load in small[:-1] + loads[::-1] + small[-1:]:
+    for load in loads[-1:] + small[:-1] + loads[-2::-1] + small[-1:]:
         load.start()
 
     barrier = pltpu.get_barrier_semaphore()
@@ -144,8 +144,13 @@
     for t, s in greeted:
         pl.semaphore_signal(barrier, inc=1, device_id={"tm": t, "space": s}, device_id_type=MESH)
 
+    def turn(r):
+        loads[r].wait()
+        obs_t[r] = obs_v[r].T
+
     for load in small[:-1]:
         load.wait()
+    turn(regions - 1)
     shape = (regions, capacity)
     which = iota2(shape, 0)
     count = jnp.zeros(shape, jnp.int32)
@@ -190,7 +195,6 @@
         return mine[block].astype(F32) + near_in[group].astype(F32)
 
     def edge_copy(group, owner, space):
-        edge_out[group] = chip_sum(group, own_block[group]).astype(BF16)
         return remote(
             edge_out.at[group],
             halo_in.at[chip],
@@ -199,10 +203,17 @@
             {"tm": owner, "space": space},
         )
 
+    edges = {FWD: edge_copy(FWD, 2 - core, after), BWD: edge_copy(BWD, 3 * core, before)}
+
+    def send_edge(group):
+        edge_out[group] = chip_sum(group, own_block[group]).astype(BF16)
+        edges[group].start()
+
     cross_copy = remote(cross_out, cross_in, cross_send, cross_recv, here(cross))
 
-    def settle(group, keep):
+    def settle(group):
         total = chip_sum(group, own_block[group])
+        keep = chip == (core if group == FAR else 1 - core)
 
         @pl.when(keep)
         def _():
@@ -218,40 +229,57 @@
     near = {g: near_copy(g, partner_block[g]) for g in (FWD, FAR, NEAR, BWD)}
 
     with jax.named_scope("p1_fwd"):
-        loads[3].wait()
-        obs_t[3] = obs_v[3].T
         gram_of(7)
-        loads[2].wait()
-        obs_t[2] = obs_v[2].T
+        turn(2)
         gram_of(6)
+
+    @pl.when(sp == 0)
+    def _():
+        turn(1)
+        turn(0)
+        for target in range(5, -1, -1):
+            gram_of(target)
+
     with jax.named_scope("p2_barrier"):
         pl.semaphore_wait(barrier, len(greeted))
-    near[FWD].start()
-    with jax.named_scope("p3_far"):
-        for r in (1, 0):
-            loads[r].wait()
-            obs_t[r] = obs_v[r].T
-        gram_of(5)
-        gram_of(4)
-    near[FAR].start()
-    with jax.named_scope("p4_fwdsum"):
-        edge_fwd = edge_copy(FWD, 2 - core, after)
-    edge_fwd.start()
-    with jax.named_scope("p5_near"):
-        gram_of(3)
-        gram_of(2)
-    near[NEAR].start()
-    with jax.named_scope("p6_farsum"):
-        settle(FAR, chip == core)
-    with jax.named_scope("p7_bwd"):
-        gram_of(1)
-        gram_of(0)
-    near[BWD].start()
-    with jax.named_scope("p8_nearsum"):
-        settle(NEAR, chip != core)
+
+    @pl.when(sp == 0)
+    def _():
+        for group in (BWD, FAR, NEAR, FWD):
+            near[group].start()
+        send_edge(BWD)
+        settle(FAR)
+        settle(NEAR)
+        send_edge(FWD)
+
+    @pl.when(sp != 0)
+    def _():
+        near[FWD].start()
+        with jax.named_scope("p3_bwd"):
+            turn(1)
+            turn(0)
+            gram_of(1)
+            gram_of(0)
+        near[BWD].start()
+        with jax.named_scope("p4_five"):
+            gram_of(5)
+        with jax.named_scope("p5_fwdsum"):
+            send_edge(FWD)
+        with jax.named_scope("p6_four"):
+            gram_of(4)
+        near[FAR].start()
+        with jax.named_scope("p7_bwdsum"):
+            send_edge(BWD)
+        with jax.named_scope("p8_near"):
+            gram_of(3)
+            gram_of(2)
+        near[NEAR].start()
+        with jax.named_scope("p9_sums"):
+            settle(FAR)
+            settle(NEAR)
 
     small[-1].wait()
-    lags, _, rows, _ = anomaly.shape
+    lags = anomaly.shape[0]
 
     def centre_on_mean(n, carry):
         lag, r = n // regions, lax.rem(n, regions)
@@ -261,9 +289,6 @@
         anomaly[lag, r] = (x - mean).astype(BF16)
         return carry
 
-    with jax.named_scope("p9_bwdsum"):
-        edge_bwd = edge_copy(BWD, 3 * core, before)
-    edge_bwd.start()
     with jax.named_scope("q0_centre"):
         lax.fori_loop(0, lags * regions, centre_on_mean, 0)
 
@@ -288,24 +313,30 @@
 
     t_cross = send_transform(0, own_slot, here(cross))
     t_near = send_transform(1, own_slot, here(partner))
-    order = [1, 0, 3, 2]
-    high = [send_transform(2 + n, 0, {"tm": t, "space": after}) for n, t in enumerate(order)]
-    low = [send_transform(2 + n, regions + 1, {"tm": t, "space": before}) for n, t in enumerate(order)]
+    to_high = lambda n, t: send_transform(2 + n, 0, {"tm": t, "space": after})
+    to_low = lambda n, t: send_transform(2 + n, regions + 1, {"tm": t, "space": before})
+    high = [to_high(n, t) for n, t in enumerate((3, 2, 1, 0))]
+    low = [to_low(n, t) for n, t in enumerate((1, 0, 3, 2))]
+    end = sp == n_space - 1
     relay = remote(t_in.at[cross_slot], t_in.at[cross_slot], t_send.at[6], t_recv.at[cross_slot], here(partner))
 
+    @pl.when(jnp.logical_and(tm == high_owner, end))
+    def _():
+        for n in (3, 2, 0, 1):
+            high[n].start()
+
     t_cross.start()
+    t_near.start()
 
     @pl.when(tm == low_owner)
     def _():
         for copy in low:
             copy.start()
 
-    @pl.when(tm == high_owner)
+    @pl.when(jnp.logical_and(tm == high_owner, jnp.logical_not(end)))
     def _():
         for copy in high:
             copy.start()
-
-    t_near.start()
 
     def place(slot, block):
         matrix, row = unpack(block.astype(F32))
@@ -313,24 +344,6 @@
 
     def wait_slot(slot):
         arrived(t_in.at[slot], t_recv.at[slot])
-
-    mid = rows // 2
-
-    def update(r, side):
-        part = slice(side * mid, (side + 1) * mid)
-        column = (iota2((mid, 1), 0) + side * mid) // (rows // HC)
-        blend = jnp.abs((column.astype(F32) + 0.5) / HC - 0.5)
-        for lag in range(lags):
-            block = anomaly[lag, r, part]
-
-            def apply(slot):
-                return lax.dot_general(
-                    block, tmat[slot], (((1,), (1,)), ((), ())), preferred_element_type=F32
-                )
-
-            centre, beside = apply(r + 1), apply(r + 2 * side)
-            mean = means[lag, r, part]
-            out_ref[lag, r, part] = (mean + centre + blend * (beside - centre)).astype(BF16)
 
     with jax.named_scope("q4_place"):
         place(own_slot, t_out[...])
@@ -344,24 +357,15 @@
         place(cross_slot, t_in[cross_slot])
         wait_slot(last_slot)
         place(last_slot, t_in[last_slot])
-    with jax.named_scope("q8_update"):
-        for r in range(regions):
-            for side in range(2):
-                if (r, side) not in ((0, 0), (regions - 1, 1)):
-                    update(r, side)
-    with jax.named_scope("q9_wait4"):
+    with jax.named_scope("q8_above"):
         wait_slot(regions + 1)
-    with jax.named_scope("r0_upd"):
         place(regions + 1, t_in[regions + 1])
-        update(regions - 1, 1)
-    with jax.named_scope("r1_wait0"):
+    with jax.named_scope("q9_below"):
         wait_slot(0)
-    with jax.named_scope("r2_upd"):
         place(0, t_in[0])
-        update(0, 0)
 
     with jax.named_scope("r3_drain"):
-        for copy in (*near.values(), edge_fwd, edge_bwd, cross_copy, t_cross, t_near, relay):
+        for copy in (*near.values(), *edges.values(), cross_copy, t_cross, t_near, relay):
             copy.wait_send()
 
         @pl.when(tm == low_owner)
@@ -373,6 +377,36 @@
         def _():
             for copy in high:
                 copy.wait_send()
+
+
+def finish(anomaly, means, tmat, out_hbm, staged, sems):
+    lags, regions, rows, _ = anomaly.shape
+    mid = rows // 2
+    copies = []
+    for r in range(regions):
+        for side in range(2):
+            part = slice(side * mid, (side + 1) * mid)
+            column = (iota2((mid, 1), 0) + side * mid) // (rows // HC)
+            blend = jnp.abs((column.astype(F32) + 0.5) / HC - 0.5)
+            for lag in range(lags):
+                block = anomaly[lag, r, part]
+
+                def apply(slot):
+                    return lax.dot_general(
+                        block, tmat[slot], (((1,), (1,)), ((), ())), preferred_element_type=F32
+                    )
+
+                centre, beside = apply(r + 1), apply(r + 2 * side)
+                mean = means[lag, r, part]
+                staged[lag, r, part] = (mean + centre + blend * (beside - centre)).astype(BF16)
+                copies.append(
+                    pltpu.make_async_copy(
+                        staged.at[lag, r, part], out_hbm.at[lag, r, part], sems.at[lag, r, side]
+                    )
+                )
+                copies[-1].start()
+    for copy in copies:
+        copy.wait()
 
 
 def shards(n_tm, n_space, obs, innovation, error_weight, obs_column, obs_count, radius, states):
@@ -384,20 +418,22 @@
     hbm = pl.BlockSpec(memory_space=pltpu.HBM)
     dma = pltpu.SemaphoreType.DMA
     packed = (rows, members)
-    result = pl.pallas_call(
+    vmem = pl.BlockSpec(memory_space=pltpu.VMEM)
+    parts = pl.pallas_call(
         functools.partial(assimilate, n_space),
-        out_shape=pltpu.VMEM(shaped.shape, BF16),
+        out_shape=[
+            pltpu.VMEM(shaped.shape, BF16),
+            pltpu.VMEM(shaped.shape[:-1] + (1,), F32),
+            pltpu.VMEM((regions + 2, members, members), BF16),
+        ],
         in_specs=[hbm] * 7,
-        out_specs=pl.BlockSpec(memory_space=pltpu.VMEM),
+        out_specs=[vmem] * 3,
         scratch_shapes=[
             pltpu.SMEM(obs_count.shape, jnp.int32),
             pltpu.SMEM(radius.shape, jnp.int32),
             pltpu.VMEM((regions, capacity), F32),
             pltpu.VMEM((regions, capacity), F32),
             pltpu.VMEM((regions, capacity), jnp.int32),
-            pltpu.VMEM(shaped.shape, BF16),
-            pltpu.VMEM(shaped.shape[:-1] + (1,), F32),
-            pltpu.VMEM((regions + 2, members, members), BF16),
             pltpu.VMEM((regions, capacity, members), BF16),
             pltpu.VMEM((regions, members, capacity), BF16),
             pltpu.VMEM((regions + 2 * HALO, *packed), BF16),
@@ -421,10 +457,19 @@
             dma((regions + 2,)),
         ],
         compiler_params=pltpu.CompilerParams(
-            collective_id=0, has_side_effects=True, vmem_limit_bytes=67043328 - 2228224
+            collective_id=0, has_side_effects=True, vmem_limit_bytes=67043328 - 5111808
         ),
         name="assimilate",
     )(obs_count, radius, obs, innovation, error_weight, obs_column, shaped)
+    result = pl.pallas_call(
+        finish,
+        out_shape=jax.ShapeDtypeStruct(shaped.shape, BF16),
+        in_specs=[vmem] * 3,
+        out_specs=hbm,
+        scratch_shapes=[pltpu.VMEM(shaped.shape, BF16), dma((lags, regions, 2))],
+        compiler_params=pltpu.CompilerParams(vmem_limit_bytes=32 << 20),
+        name="finish",
+    )(*parts)
     return result.reshape(states.shape)
 
 

time: 26 us -> 23.2 us (0.89)
  the two profiles are of different devices: /device:TPU:0 before, /device:TPU:1 now
where the time goes in v2:
time: 23.2 us; the launch traced here: 23 us
  Pallas kernels  23 us (99%)
    pallas_call x1, Pallas kernels, shards(): pl.pallas_call(functools.partial(assimilate, n_space), out_shape=[pltpu.V...  20.9 us
    pallas_call x1, Pallas kernels, shards(): pl.pallas_call(finish, out_shape=jax.ShapeDtypeStruct(shaped.shape, BF16)...  2.1 us

profile of v2, /device:TPU:1, one launch (start us, length us, event | category | flops | bytes accessed | tf_op | source)
XLA Modules:
  0.0 23.0 jit_solution(9786733329264543470)
XLA Ops:
  0.0 20.9 %assimilate.1 = (bf16[2,4,512,256]{3,2,1,0:T(8,128)(2,1)S(1)}, f32[2,4,512,1]{3,2,1,0:T(8,128)S(1)}, bf16[6,256,256]{2,1,0:T(8,128)(2,1)S(1)}) custom-call(s32[1,4]{1,0:T(1,128)} %count_hbm.1, s32[4]{0:T(128)} %radius_hbm.1, bf16[1,4,1024,256]{3,2,1,0:T(8,128)(2,1)} %obs_hbm.1, f32[1,4,1024]{2,1,0:T(4,128)} %innov_hbm.1, f32[1,4,1024]{2,1,0:T(4,128)} %weight_hbm.1, ...), custom_call_target="tpu_custom_call" | custom-call | tf_op jit(solution)/shard_map/assimilate/pallas_call | solution.py:422
  20.9 2.1 %finish.1 = bf16[2,4,512,256]{3,2,1,0:T(8,128)(2,1)} custom-call(bf16[2,4,512,256]{3,2,1,0:T(8,128)(2,1)S(1)} %get-tuple-element.8.anomaly, f32[2,4,512,1]{3,2,1,0:T(8,128)S(1)} %get-tuple-element.9.means, bf16[6,256,256]{2,1,0:T(8,128)(2,1)S(1)} %get-tuple-element.10.tmat), custom_call_target="tpu_custom_call" | custom-call | tf_op jit(solution)/shard_map/finish/pallas_call | solution.py:464

commit v3 on v2

--- a/solution.py
+++ b/solution.py
@@ -49,33 +49,40 @@
     return matrix, row
 
 
-def transform_parts(gram, vec):
+def transform_parts(gram, vec, shift):
     n = gram.shape[0]
     both = lambda x: jnp.sum(jnp.sum(x, axis=0, keepdims=True), axis=1, keepdims=True)
     identity = (iota2(gram.shape, 0) == iota2(gram.shape, 1)).astype(F32)
-    system = gram + (n - 1) / INFLATION * identity
-    frob = jnp.sqrt(both(system * system))
-    inverse_frob = 1.0 / frob
-    a = both(system * identity) * (1.0 / n) * inverse_frob
-    rest = system * inverse_frob - a * identity
+    base = (n - 1) / INFLATION
+    rest = gram - shift * identity
+    r = rest.astype(BF16)
     u = jnp.broadcast_to(vec, (EXTRA, n))
     dot = functools.partial(jnp.dot, preferred_element_type=F32)
-    z_one = z_rest = None
-    for step in range(NS_ITERS):
+    first = dot(jnp.concatenate([r, u.astype(BF16)], axis=0), r)
+    system = gram + base * identity
+    frob = jnp.sqrt(both(system * system))
+    unit = 1.0 / frob
+    a = (shift + base) * unit
+    h = 1.5 - 0.5 * a
+    turned = h * u - (0.5 * unit) * first[n:]
+    second = dot(jnp.concatenate([first[:n].astype(BF16), turned.astype(BF16)], axis=0), r)
+    u = h * turned - (0.5 * unit) * second[n:]
+    z_rest, z_one = (-0.5 * unit) * rest, h
+    rest = (
+        ((2.25 - 3.0 * a + 0.75 * a * a) * unit) * rest
+        + ((0.75 * a - 1.5) * unit * unit) * first[:n]
+        + (0.25 * unit * unit * unit) * second[:n]
+    )
+    a = a * h * h
+    for step in range(1, NS_ITERS):
         last = step == NS_ITERS - 1
         h = 1.5 - 0.5 * a
         r = rest.astype(BF16)
-        left = [] if last else [r]
-        if step:
-            left.append(z_rest.astype(BF16))
-        left.append(u.astype(BF16))
-        first = dot(jnp.concatenate(left, axis=0), r)
+        left = [z_rest.astype(BF16), u.astype(BF16)]
+        first = dot(jnp.concatenate(left if last else [r, *left], axis=0), r)
         turned = h * u - 0.5 * first[-EXTRA:]
-        if step:
-            z_rest = h * z_rest - (0.5 * z_one) * rest - 0.5 * first[-EXTRA - n : -EXTRA]
-            z_one = h * z_one
-        else:
-            z_rest, z_one = -0.5 * rest, h
+        z_rest = h * z_rest - (0.5 * z_one) * rest - 0.5 * first[-EXTRA - n : -EXTRA]
+        z_one = h * z_one
         left = [] if last else [first[:n].astype(BF16)]
         left.append(turned.astype(BF16))
         second = dot(jnp.concatenate(left, axis=0), r)
@@ -89,12 +96,23 @@
             a = a * h * h
     scale = jnp.sqrt(F32(n - 1.0)) * lax.rsqrt(frob)
     spread = (z_rest + z_one * identity) * scale
-    return spread, u[0:1] * inverse_frob
+    return spread, u[0:1] * unit
+
+
+def blended(block, mean, centre, beside, side):
+    mid = block.shape[0]
+    column = (iota2((mid, 1), 0) + side * mid) // (2 * mid // HC)
+    blend = jnp.abs((column.astype(F32) + 0.5) / HC - 0.5)
+    apply = lambda t: lax.dot_general(
+        block, t, (((1,), (1,)), ((), ())), preferred_element_type=F32
+    )
+    own, other = apply(centre), apply(beside)
+    return (mean + own + blend * (other - own)).astype(BF16)
 
 
 def assimilate(
     n_space,
-    count_hbm, radius_hbm, obs_hbm, innov_hbm, weight_hbm, column_hbm, states_hbm, anomaly, means, tmat,
+    count_hbm, radius_hbm, obs_hbm, innov_hbm, weight_hbm, column_hbm, states_hbm, done, anomaly, means, tmat,
     count_ref, radius_ref, innov_ref, weight_ref, column_ref, obs_v, obs_t,
     mine, near_in, edge_out, halo_in, own, cross_out, cross_in, t_out, t_in,
     load_sem, small_sem, near_send, near_recv, edge_send, halo_recv, cross_send, cross_recv,
@@ -106,8 +124,7 @@
     partner, cross = 2 * chip + 1 - core, 2 * (1 - chip) + core
     regions, capacity, members = obs_v.shape
     half = members // 2
-    region_of = lambda t: lax.rem(t + 2, 3) + t // 3
-    low_owner, high_owner = 1, 3
+    region_of = lambda x, c: (1 - x) * (1 - c) + x * (2 + c)
     here = lambda t: {"tm": t, "space": sp}
 
     def remote(src, dst, send, recv, device):
@@ -117,6 +134,22 @@
 
     def arrived(ref, sem):
         pltpu.make_async_copy(ref, ref, sem).wait()
+
+    barrier = pltpu.get_barrier_semaphore()
+    first, end = sp == 0, sp == n_space - 1
+    low_owner, high_owner = 1, 3
+    greet = lambda t, s: pl.semaphore_signal(
+        barrier, inc=1, device_id={"tm": t, "space": s}, device_id_type=MESH
+    )
+    sender_space = jnp.where(chip == 0, before, after)
+    greet(partner, sp)
+    greet(cross, sp)
+    greet(core, sender_space)
+    greet(core + 2, sender_space)
+
+    @pl.when(jnp.logical_and(first, tm == 0))
+    def _():
+        greet(high_owner, before)
 
     loads = [
         pltpu.make_async_copy(obs_hbm.at[0, r], obs_v.at[r], load_sem.at[r]) for r in range(regions)
@@ -136,13 +169,6 @@
     ]
     for load in loads[-1:] + small[:-1] + loads[-2::-1] + small[-1:]:
         load.start()
-
-    barrier = pltpu.get_barrier_semaphore()
-    peers = [lax.rem(tm + d, 4) for d in range(1, 4)]
-    greeted = [(p, sp) for p in peers]
-    greeted += [(t, s) for s in (before, after) for t in range(4)]
-    for t, s in greeted:
-        pl.semaphore_signal(barrier, inc=1, device_id={"tm": t, "space": s}, device_id_type=MESH)
 
     def turn(r):
         loads[r].wait()
@@ -203,7 +229,7 @@
             {"tm": owner, "space": space},
         )
 
-    edges = {FWD: edge_copy(FWD, 2 - core, after), BWD: edge_copy(BWD, 3 * core, before)}
+    edges = {FWD: edge_copy(FWD, core, after), BWD: edge_copy(BWD, 2 + core, before)}
 
     def send_edge(group):
         edge_out[group] = chip_sum(group, own_block[group]).astype(BF16)
@@ -213,7 +239,7 @@
 
     def settle(group):
         total = chip_sum(group, own_block[group])
-        keep = chip == (core if group == FAR else 1 - core)
+        keep = chip == (1 if group == FAR else 0)
 
         @pl.when(keep)
         def _():
@@ -233,7 +259,7 @@
         turn(2)
         gram_of(6)
 
-    @pl.when(sp == 0)
+    @pl.when(first)
     def _():
         turn(1)
         turn(0)
@@ -241,18 +267,23 @@
             gram_of(target)
 
     with jax.named_scope("p2_barrier"):
-        pl.semaphore_wait(barrier, len(greeted))
-
-    @pl.when(sp == 0)
+        pl.semaphore_wait(barrier, jnp.where(jnp.logical_and(end, tm == high_owner), 5, 4))
+
+
+    @pl.when(first)
     def _():
         for group in (BWD, FAR, NEAR, FWD):
             near[group].start()
-        send_edge(BWD)
+
+        @pl.when(core == 1)
+        def _():
+            send_edge(BWD)
+
         settle(FAR)
         settle(NEAR)
         send_edge(FWD)
 
-    @pl.when(sp != 0)
+    @pl.when(jnp.logical_not(first))
     def _():
         near[FWD].start()
         with jax.named_scope("p3_bwd"):
@@ -261,25 +292,26 @@
             gram_of(1)
             gram_of(0)
         near[BWD].start()
-        with jax.named_scope("p4_five"):
+        with jax.named_scope("p4_fwdsum"):
+            send_edge(FWD)
+        with jax.named_scope("p5_far"):
             gram_of(5)
-        with jax.named_scope("p5_fwdsum"):
-            send_edge(FWD)
-        with jax.named_scope("p6_four"):
             gram_of(4)
         near[FAR].start()
-        with jax.named_scope("p7_bwdsum"):
+        with jax.named_scope("p6_bwdsum"):
             send_edge(BWD)
-        with jax.named_scope("p8_near"):
+        with jax.named_scope("p7_near"):
             gram_of(3)
             gram_of(2)
         near[NEAR].start()
-        with jax.named_scope("p9_sums"):
+        with jax.named_scope("p8_farsum"):
             settle(FAR)
+        with jax.named_scope("p9_nearsum"):
             settle(NEAR)
 
     small[-1].wait()
-    lags = anomaly.shape[0]
+    lags, _, rows, _ = anomaly.shape
+    mid = rows // 2
 
     def centre_on_mean(n, carry):
         lag, r = n // regions, lax.rem(n, regions)
@@ -292,21 +324,29 @@
     with jax.named_scope("q0_centre"):
         lax.fori_loop(0, lags * regions, centre_on_mean, 0)
 
+    @pl.when(jnp.logical_and(first, core == 0))
+    def _():
+        send_edge(BWD)
+
     with jax.named_scope("q1_cross"):
         arrived(cross_in, cross_recv)
+        total = own[...] + cross_in[...].astype(F32)
+        corner, extra = total[:half, half:], total[half + 1 : half + 2, :half]
+        corner = jnp.where(iota2((half, half), 0) == iota2((half, half), 1), corner, 0.0)
+        diagonal = jnp.sum(corner, axis=0, keepdims=True) + extra
+        shift = jnp.sum(diagonal, axis=1, keepdims=True) * (1.0 / members)
     with jax.named_scope("q2_halo"):
         for x in range(2):
             arrived(halo_in.at[x], halo_recv.at[x])
     with jax.named_scope("q3_ns"):
-        total = own[...] + cross_in[...].astype(F32)
         gram, vec = unpack(total + (halo_in[0].astype(F32) + halo_in[1].astype(F32)))
-        spread, wbar = transform_parts(gram, vec)
+        spread, wbar = transform_parts(gram, vec, shift)
         top, extra = pack(spread, wbar)
         t_out[:half] = top.astype(BF16)
         t_out[half:] = extra.astype(BF16)
 
-    own_slot, cross_slot = region_of(tm) + 1, region_of(cross) + 1
-    near_slot, last_slot = region_of(partner) + 1, region_of(2 * (1 - chip) + 1 - core) + 1
+    own_slot, cross_slot = region_of(chip, core) + 1, region_of(1 - chip, core) + 1
+    near_slot, last_slot = region_of(chip, 1 - core) + 1, region_of(1 - chip, 1 - core) + 1
 
     def send_transform(n, slot, device):
         return remote(t_out, t_in.at[slot], t_send.at[n], t_recv.at[slot], device)
@@ -315,25 +355,30 @@
     t_near = send_transform(1, own_slot, here(partner))
     to_high = lambda n, t: send_transform(2 + n, 0, {"tm": t, "space": after})
     to_low = lambda n, t: send_transform(2 + n, regions + 1, {"tm": t, "space": before})
-    high = [to_high(n, t) for n, t in enumerate((3, 2, 1, 0))]
-    low = [to_low(n, t) for n, t in enumerate((1, 0, 3, 2))]
-    end = sp == n_space - 1
-    relay = remote(t_in.at[cross_slot], t_in.at[cross_slot], t_send.at[6], t_recv.at[cross_slot], here(partner))
-
-    @pl.when(jnp.logical_and(tm == high_owner, end))
-    def _():
-        for n in (3, 2, 0, 1):
-            high[n].start()
+    high = [to_high(n, t) for n, t in enumerate((3, 1))]
+    far_end = to_high(2, 0)
+    low = [to_low(n, t) for n, t in enumerate((1, 3))]
+    pass_on = lambda n, slot: remote(
+        t_in.at[slot], t_in.at[slot], t_send.at[n], t_recv.at[slot], here(partner)
+    )
+    relay, relay_above, relay_below = pass_on(6, cross_slot), pass_on(7, regions + 1), pass_on(8, 0)
+    served = jnp.logical_and(first, chip == 0)
+    is_low, is_high = tm == low_owner, tm == high_owner
+
+    @pl.when(jnp.logical_and(is_high, end))
+    def _():
+        for copy in (far_end, high[1], high[0]):
+            copy.start()
 
     t_cross.start()
     t_near.start()
 
-    @pl.when(tm == low_owner)
+    @pl.when(is_low)
     def _():
         for copy in low:
             copy.start()
 
-    @pl.when(jnp.logical_and(tm == high_owner, jnp.logical_not(end)))
+    @pl.when(jnp.logical_and(is_high, jnp.logical_not(end)))
     def _():
         for copy in high:
             copy.start()
@@ -350,61 +395,114 @@
     with jax.named_scope("q5_near"):
         wait_slot(near_slot)
         place(near_slot, t_in[near_slot])
-    with jax.named_scope("q6_cross"):
+    def boundary(b):
+        for lag in range(lags):
+            for r, side in ((b, 1), (b + 1, 0)):
+                part = slice(side * mid, (side + 1) * mid)
+                done[lag, r, part] = blended(
+                    anomaly[lag, r, part], means[lag, r, part], tmat[r + 1], tmat[r + 2 * side], side
+                )
+
+    with jax.named_scope("q6_bound1"):
+        boundary(2 * chip)
+    with jax.named_scope("q7_cross"):
         wait_slot(cross_slot)
-    relay.start()
-    with jax.named_scope("q7_last"):
+        relay.start()
         place(cross_slot, t_in[cross_slot])
+
+    @pl.when(core == 1)
+    def _():
+        with jax.named_scope("q8_relays"):
+            wait_slot(regions + 1)
+            relay_above.start()
+
+            @pl.when(jnp.logical_not(served))
+            def _():
+                wait_slot(0)
+                relay_below.start()
+
+    with jax.named_scope("q8_bound2"):
+
+        @pl.when(core == 0)
+        def _():
+            boundary(1)
+
+    with jax.named_scope("q9_last"):
         wait_slot(last_slot)
         place(last_slot, t_in[last_slot])
-    with jax.named_scope("q8_above"):
-        wait_slot(regions + 1)
+    with jax.named_scope("r0_bound3"):
+
+        @pl.when(core == 1)
+        def _():
+            boundary(1)
+
+        boundary(2 - 2 * chip)
+
+    with jax.named_scope("r1_above"):
+
+        @pl.when(core == 0)
+        def _():
+            wait_slot(regions + 1)
+
         place(regions + 1, t_in[regions + 1])
-    with jax.named_scope("q9_below"):
-        wait_slot(0)
+    with jax.named_scope("r2_below"):
+
+        @pl.when(jnp.logical_or(core == 0, served))
+        def _():
+            wait_slot(0)
+
         place(0, t_in[0])
 
     with jax.named_scope("r3_drain"):
         for copy in (*near.values(), *edges.values(), cross_copy, t_cross, t_near, relay):
             copy.wait_send()
 
-        @pl.when(tm == low_owner)
+        @pl.when(core == 1)
+        def _():
+            relay_above.wait_send()
+
+            @pl.when(jnp.logical_not(served))
+            def _():
+                relay_below.wait_send()
+
+        @pl.when(is_low)
         def _():
             for copy in low:
                 copy.wait_send()
 
-        @pl.when(tm == high_owner)
+        @pl.when(is_high)
         def _():
             for copy in high:
                 copy.wait_send()
 
-
-def finish(anomaly, means, tmat, out_hbm, staged, sems):
+            @pl.when(end)
+            def _():
+                far_end.wait_send()
+
+
+def finish(done, anomaly, means, tmat, out_hbm, outer, sems):
     lags, regions, rows, _ = anomaly.shape
     mid = rows // 2
     copies = []
-    for r in range(regions):
-        for side in range(2):
-            part = slice(side * mid, (side + 1) * mid)
-            column = (iota2((mid, 1), 0) + side * mid) // (rows // HC)
-            blend = jnp.abs((column.astype(F32) + 0.5) / HC - 0.5)
-            for lag in range(lags):
-                block = anomaly[lag, r, part]
-
-                def apply(slot):
-                    return lax.dot_general(
-                        block, tmat[slot], (((1,), (1,)), ((), ())), preferred_element_type=F32
-                    )
-
-                centre, beside = apply(r + 1), apply(r + 2 * side)
-                mean = means[lag, r, part]
-                staged[lag, r, part] = (mean + centre + blend * (beside - centre)).astype(BF16)
-                copies.append(
-                    pltpu.make_async_copy(
-                        staged.at[lag, r, part], out_hbm.at[lag, r, part], sems.at[lag, r, side]
-                    )
-                )
-                copies[-1].start()
+
+    def put(src, lag, r, side):
+        dst = out_hbm.at[lag, r, slice(side * mid, (side + 1) * mid)]
+        copies.append(pltpu.make_async_copy(src, dst, sems.at[lag, r, side]))
+        copies[-1].start()
+
+    ends = ((0, 0), (regions - 1, 1))
+    for lag in range(lags):
+        for r in range(regions):
+            for side in range(2):
+                if (r, side) not in ends:
+                    put(done.at[lag, r, slice(side * mid, (side + 1) * mid)], lag, r, side)
+    for r, side in ends:
+        part = slice(side * mid, (side + 1) * mid)
+        for lag in range(lags):
+            outer[lag, side] = blended(
+                anomaly[lag, r, part], means[lag, r, part], tmat[r + 1], tmat[r + 2 * side], side
+            )
+            put(outer.at[lag, side], lag, r, side)
     for copy in copies:
         copy.wait()
 
@@ -423,11 +521,12 @@
         functools.partial(assimilate, n_space),
         out_shape=[
             pltpu.VMEM(shaped.shape, BF16),
+            pltpu.VMEM(shaped.shape, BF16),
             pltpu.VMEM(shaped.shape[:-1] + (1,), F32),
             pltpu.VMEM((regions + 2, members, members), BF16),
         ],
         in_specs=[hbm] * 7,
-        out_specs=[vmem] * 3,
+        out_specs=[vmem] * 4,
         scratch_shapes=[
             pltpu.SMEM(obs_count.shape, jnp.int32),
             pltpu.SMEM(radius.shape, jnp.int32),
@@ -453,20 +552,23 @@
             dma((2,)),
             dma,
             dma,
-            dma((7,)),
+            dma((9,)),
             dma((regions + 2,)),
         ],
         compiler_params=pltpu.CompilerParams(
-            collective_id=0, has_side_effects=True, vmem_limit_bytes=67043328 - 5111808
+            collective_id=0, has_side_effects=True, vmem_limit_bytes=67043328 - 7208960
         ),
         name="assimilate",
     )(obs_count, radius, obs, innovation, error_weight, obs_column, shaped)
     result = pl.pallas_call(
         finish,
         out_shape=jax.ShapeDtypeStruct(shaped.shape, BF16),
-        in_specs=[vmem] * 3,
+        in_specs=[vmem] * 4,
         out_specs=hbm,
-        scratch_shapes=[pltpu.VMEM(shaped.shape, BF16), dma((lags, regions, 2))],
+        scratch_shapes=[
+            pltpu.VMEM((lags, 2, shaped.shape[2] // 2, members), BF16),
+            dma((lags, regions, 2)),
+        ],
         compiler_params=pltpu.CompilerParams(vmem_limit_bytes=32 << 20),
         name="finish",
     )(*parts)

time: 23.2 us -> 22.4 us (0.966)
  Pallas kernels: 23 us -> 22.2 us
    pallas_call x1, Pallas kernels: 2.1 us -> 1.45 us  [shards(): pl.pallas_call(finish, out_shape=jax.ShapeDtypeStruct(shaped.shape, BF16)...]
where the time goes in v3:
time: 22.4 us; the launch traced here: 22.3 us
  Pallas kernels  22.2 us (99%)
    pallas_call x1, Pallas kernels, shards(): pl.pallas_call(functools.partial(assimilate, n_space), out_shape=[pltpu.V...  20.8 us
    pallas_call x1, Pallas kernels, shards(): pl.pallas_call(finish, out_shape=jax.ShapeDtypeStruct(shaped.shape, BF16)...  1.45 us

profile of v3, /device:TPU:1, one launch (start us, length us, event | category | flops | bytes accessed | tf_op | source)
XLA Modules:
  0.0 22.3 jit_solution(16198398212835865024)
XLA Ops:
  0.0 20.8 %assimilate.1 = (bf16[2,4,512,256]{3,2,1,0:T(8,128)(2,1)S(1)}, bf16[2,4,512,256]{3,2,1,0:T(8,128)(2,1)S(1)}, f32[2,4,512,1]{3,2,1,0:T(8,128)S(1)}, bf16[6,256,256]{2,1,0:T(8,128)(2,1)S(1)}) custom-call(s32[1,4]{1,0:T(1,128)} %count_hbm.1, s32[4]{0:T(128)} %radius_hbm.1, bf16[1,4,1024,256]{3,2,1,0:T(8,128)(2,1)} %obs_hbm.1, f32[1,4,1024]{2,1,0:T(4,128)} %innov_hbm.1, ...), custom_call_target="tpu_custom_call" | custom-call | tf_op jit(solution)/shard_map/assimilate/pallas_call | solution.py:520
  20.8 1.4 %finish.1 = bf16[2,4,512,256]{3,2,1,0:T(8,128)(2,1)} custom-call(bf16[2,4,512,256]{3,2,1,0:T(8,128)(2,1)S(1)} %get-tuple-element.9.done, bf16[2,4,512,256]{3,2,1,0:T(8,128)(2,1)S(1)} %get-tuple-element.10.anomaly, f32[2,4,512,1]{3,2,1,0:T(8,128)S(1)} %get-tuple-element.11.means, bf16[6,256,256]{2,1,0:T(8,128)(2,1)S(1)} %get-tuple-element.12.tmat), custom_call_target="tpu_custom_call" | custom-call | tf_op jit(solution)/shard_map/finish/pallas_call | solution.py:563
